TPU v7x, 32 devices: a whole 2x2x4 slice. The times are simulated.
32 devices in a mesh: row: 8 (over z, y), col: 4 (over x, core).
Axes of the slice: x: 2, y: 2, z: 4, core: 2. Of those that a mesh axis runs over, the one named last changes fastest.
Arguments:
- layer_input: bfloat16 [2048, 8192], P('row'), may hold values from -7 to 7
- gain: float32 [8192], replicated, may hold values from 0.5 to 6
- d_query: bfloat16 [2048, 4096], P('row', 'col'), may hold values from -6 to 6
- d_keyval: bfloat16 [2048, 2048], P('row', 'col'), may hold values from -6 to 6
- w_query: bfloat16 [8192, 4096], P('row', 'col'), may hold values from -0.0625 to 0.0625
- w_keyval: bfloat16 [8192, 2048], P('row', 'col'), may hold values from -1 to 1
- d_resid: bfloat16 [2048, 8192], P('row', 'col'), may hold values from -6 to 6
Outputs:
- d_input: bfloat16 [2048, 8192], P('row', 'col')
- grad_wq: bfloat16 [8192, 4096], P('row', 'col')
- grad_wkv: bfloat16 [8192, 2048], P('row', 'col')
- grad_gain: float32 [8192], P('col')
- grad_square_sum: float32 [], replicated
All inputs are finite; a program needn't handle non-finite values.
Results may differ from a plain program's by a relative error of at most 0.023.
Values may be sent and summed in bfloat16 or wider, within the bound.
A program may use at most 128 MiB of HBM per device.

v0:
```python
import math
import jax
import jax.numpy as jnp
from jax import lax
from jax.sharding import PartitionSpec as P

epsilon = 1e-05


def local(layer_input, gain, d_query, d_keyval, w_query, w_keyval, d_resid):
    inputs = layer_input.astype(jnp.float32)
    inv_rms = lax.rsqrt(jnp.mean(inputs * inputs, axis=1, keepdims=True) + epsilon)
    normed = (inputs * inv_rms * gain).astype(jnp.bfloat16)
    model_width = inputs.shape[1]
    local_tokens = inputs.shape[0]
    tokens_all = local_tokens * lax.axis_size("row")
    scaling = 1.0 / math.sqrt(tokens_all)
    weight_scale = 1.0 / math.sqrt(local_tokens)
    contract_cols = (((1,), (1,)), ((), ()))
    partial_value = lax.dot_general(
        d_query,
        lax.all_gather(w_query, "row", axis=0, tiled=True),
        contract_cols,
        preferred_element_type=jnp.float32,
    )
    partial_value = partial_value + lax.dot_general(
        d_keyval,
        lax.all_gather(w_keyval, "row", axis=0, tiled=True),
        contract_cols,
        preferred_element_type=jnp.float32,
    )
    rounded = lax.optimization_barrier(partial_value.astype(jnp.bfloat16)).astype(jnp.float32)
    feature_grad = lax.psum_scatter(
        rounded.astype(jnp.bfloat16), "col", scatter_dimension=1, tiled=True
    ).astype(jnp.float32)
    slice_width = feature_grad.shape[1]
    col_start = lax.axis_index("col") * slice_width
    input_part = lax.dynamic_slice_in_dim(inputs, col_start, slice_width, 1)
    gain_part = lax.dynamic_slice_in_dim(gain, col_start, slice_width, 0)
    weighted = gain_part * feature_grad
    token_dot = lax.psum(jnp.sum(weighted * input_part, axis=1, keepdims=True), "col")
    d_input = (
        d_resid.astype(jnp.float32)
        + inv_rms * weighted
        - input_part * inv_rms**3 * token_dot / model_width
    ).astype(jnp.bfloat16)
    gain_partial = jnp.sum(feature_grad * input_part * inv_rms, axis=0) * scaling
    cotangent = jnp.concatenate([d_query, d_keyval], axis=1)
    query_cols = d_query.shape[1]
    columns = lax.all_to_all(normed, "row", split_axis=1, concat_axis=0, tiled=True)
    all_cotangents = lax.all_gather(cotangent, "row", axis=0, tiled=True)
    groups = lax.axis_size("row")
    column_blocks = columns.reshape(groups, local_tokens, columns.shape[1])
    grad_blocks = all_cotangents.reshape(groups, local_tokens, all_cotangents.shape[1])
    blocks = (
        lax.dot_general(
            column_blocks,
            grad_blocks,
            (((1,), (1,)), ((0,), (0,))),
            preferred_element_type=jnp.float32,
        )
        * weight_scale
    )
    summed = jnp.sum(blocks.astype(jnp.bfloat16).astype(jnp.float32), axis=0)
    grad_wq = summed[:, :query_cols].astype(jnp.bfloat16)
    grad_wkv = summed[:, query_cols:].astype(jnp.bfloat16)
    query_f = grad_wq.astype(jnp.float32)
    keyval_f = grad_wkv.astype(jnp.float32)
    tile_square = jnp.sum(query_f * query_f) + jnp.sum(keyval_f * keyval_f)
    grad_gain = lax.psum(gain_partial, "row")
    leading = jnp.where(
        lax.axis_index("row") == 0, jnp.sum(grad_gain * grad_gain), jnp.float32(0.0)
    )
    grand_total = lax.psum(tile_square + leading, ("row", "col"))
    grad_square_sum = grand_total / jnp.float32(model_width)
    return (d_input, grad_wq, grad_wkv, grad_gain, grad_square_sum)


def solution(mesh):
    placed = (
        P("row", None),
        P(),
        P("row", "col"),
        P("row", "col"),
        P("row", "col"),
        P("row", "col"),
        P("row", "col"),
    )
    return jax.shard_map(
        local,
        mesh=mesh,
        in_specs=placed,
        out_specs=(P("row", "col"), P("row", "col"), P("row", "col"), P("col"), P()),
        check_vma=False,
    )
```

profile of v0, /device:TPU:12, one launch (start us, length us, event | category | flops | bytes accessed | tf_op | source)
XLA Modules:
  0.0 671.1 jit_solution(14180824158022452798)
XLA Ops:
  7.2 0.0 all-gather.6.cloned.1.call-start
  7.2 0.7 all-gather.6.cloned.1.call-update
  7.9 0.0 copy-start.4
  7.9 0.0 all-gather.4.cloned.1.call-start
  8.0 0.7 all-gather.4.cloned.1.call-update
  8.7 0.0 all-gather.8.cloned.1.call-start
  8.7 2.1 pad_maximum_fusion
  10.8 0.0 all-gather.8.cloned.1.call-update
  10.8 0.0 copy-start
  10.8 3.3 multiply_reduce_fusion
  14.1 0.0 copy-done.4
  14.1 0.2 copy-done
  14.2 3.2 multiply_convert_fusion.1
  17.4 6.5 copy.13
  23.9 0.0 copy-start.2
  23.9 6.4 all-to-all-start
  30.3 0.0 copy-start.1
  30.3 0.0 reduce-scatter.2.cloned.1.call-start
  30.3 181.7 %all-gather.6.cloned.1.call-done = bf16[8192,512]{1,0:T(8,128)(2,1)} async-done(((bf16[1024,512]{1,0:T(8,128)(2,1)}), bf16[8192,512]{1,0:T(8,128)(2,1)}) %all-gather.6.cloned.1.call-update) | async-done | bytes 8388624 | tf_op jit(solution)/shard_map/all_gather | solution.py:28
  212.0 0.0 copy-done.2
  212.1 9.0 %fusion.11 = f32[256,8192]{1,0:T(8,128)} fusion(bf16[256,512]{1,0:T(8,128)(2,1)S(1)} %copy-done.2, bf16[8192,512]{1,0:T(8,128)(2,1)} %all-gather.6.cloned.1.call-done), kind=kOutput, calls=%fused_computation.24 | convolution fusion | flops 2147483648 | bytes 17039360 | tf_op jit(solution)/shard_map/dot_general | solution.py:26
  221.0 219.9 %all-gather.4.cloned.1.call-done = bf16[8192,1024]{1,0:T(8,128)(2,1)} async-done(((bf16[1024,1024]{1,0:T(8,128)(2,1)}), bf16[8192,1024]{1,0:T(8,128)(2,1)}) %all-gather.4.cloned.1.call-update) | async-done | bytes 16777232 | tf_op jit(solution)/shard_map/all_gather | solution.py:22
  440.9 0.0 copy-done.1
  440.9 12.4 %fusion = bf16[256,8192]{1,0:T(8,128)(2,1)} fusion(f32[256,8192]{1,0:T(8,128)} %fusion.11, bf16[256,1024]{1,0:T(8,128)(2,1)S(1)} %copy-done.1, bf16[8192,1024]{1,0:T(8,128)(2,1)} %all-gather.4.cloned.1.call-done), kind=kOutput, calls=%fused_computation.2 | convolution fusion | flops 4299161600 | bytes 29884416 | tf_op jit(solution)/shard_map/dot_general | solution.py:20
  453.4 0.0 reduce-scatter.2.cloned.1.call-update
  453.4 6.7 convert_element_type.35
  460.0 0.0 all-to-all-done
  460.0 81.3 %all-gather.8.cloned.1.call-done = bf16[2048,1536]{1,0:T(8,128)(2,1)} async-done(((bf16[256,1536]{1,0:T(8,128)(2,1)}), bf16[2048,1536]{1,0:T(8,128)(2,1)}) %all-gather.8.cloned.1.call-update) | async-done | bytes 6291472 | tf_op jit(solution)/shard_map/all_gather | solution.py:51
  541.3 10.9 %fusion.1 = bf16[1024,1536]{1,0:T(8,128)(2,1)S(1)} fusion(bf16[8,256,1536]{2,1,0:T(8,128)(2,1)} %bitcast.11, bf16[256,8,1024]{0,2,1:T(8,128)(2,1)} %all-to-all-done), kind=kOutput, calls=%fused_computation.5 | convolution fusion | flops 6478626816 | bytes 13631488 | tf_op jit(solution)/shard_map/dot_general | solution.py:56
  552.2 2.0 multiply_reduce_fusion.2
  554.3 0.0 copy-start.3
  554.3 2.9 multiply_reduce_fusion.1
  558.5 29.9 %reduce-scatter.2.cloned.1.call-done = bf16[256,2048]{1,0:T(8,128)(2,1)} async-done(((bf16[256,8192]{1,0:T(8,128)(2,1)}), bf16[256,2048]{1,0:T(8,128)(2,1)}) %reduce-scatter.2.cloned.1.call-update) | async-done | bytes 1048592 | tf_op jit(solution)/shard_map/reduce_scatter | solution.py:33
  588.4 2.6 fusion.10
  591.0 15.3 %psum.22 = f32[2048]{0:T(1024)S(1)} all-reduce(f32[2048]{0:T(1024)S(1)} %broadcast_multiply_fusion), channel_id=1, replica_groups=mesh['row'=8,'col'=4] {'row'}, use_global_device_ids=true, to_apply=%region_6.0 | all-reduce | flops 2048 | bytes 16384 | tf_op jit(solution)/shard_map/psum | solution.py:70
  606.3 0.0 copy-start.5
  606.3 0.6 multiply_reduce_fusion.3
  607.5 6.0 psum.21
  613.5 45.6 %psum.23 = f32[]{:T(128)} all-reduce(f32[]{:T(128)S(6)} %add.44), channel_id=1, replica_groups=mesh['row'=8,'col'=4] {'row','col'}, use_global_device_ids=true, to_apply=%region_10.11 | all-reduce | flops 1 | bytes 8 | tf_op jit(solution)/shard_map/psum | solution.py:74
  659.7 0.0 copy-done.3
  659.8 3.6 fusion.7
  663.4 0.0 copy-done.5
  (3 shorter events, 0.0 us)
Async XLA Ops:
  7.2 204.9 %all-gather.6.cloned.1.call-start = ((), (), s32[]{:S(2)}) async-start(), calls=%async_computation.3 | async-start | bytes 9437184 | tf_op jit(solution)/shard_map/all_gather | solution.py:28
  7.9 6.2 copy-start.4
  7.9 433.0 %all-gather.4.cloned.1.call-start = ((), (), s32[]{:S(2)}) async-start(), calls=%async_computation.2 | async-start | bytes 18874368 | tf_op jit(solution)/shard_map/all_gather | solution.py:22
  8.7 532.6 %all-gather.8.cloned.1.call-start = ((), (), s32[]{:S(2)}) async-start(), calls=%async_computation.5 | async-start | bytes 7077888 | tf_op jit(solution)/shard_map/all_gather | solution.py:51
  10.8 3.5 copy-start
  23.9 188.1 %copy-start.2 = (bf16[256,512]{1,0:T(8,128)(2,1)S(1)}, bf16[256,512]{1,0:T(8,128)(2,1)}, u32[]{:S(2)}) copy-start(bf16[256,512]{1,0:T(8,128)(2,1)} %param.10) | copy-start | bytes 786436
  23.9 436.1 %all-to-all-start = ((bf16[256,8,1024]{0,2,1:T(8,128)(2,1)}), bf16[256,8,1024]{0,2,1:T(8,128)(2,1)}, u32[]{:S(2)}, u32[]{:S(2)}) async-start(bf16[256,8,1024]{0,2,1:T(8,128)(2,1)} %bitcast.10), calls=%async_computation.1 | async-start | bytes 8388608 | tf_op jit(solution)/shard_map/all_to_all | solution.py:50
  30.3 410.6 %copy-start.1 = (bf16[256,1024]{1,0:T(8,128)(2,1)S(1)}, bf16[256,1024]{1,0:T(8,128)(2,1)}, u32[]{:S(2)}) copy-start(bf16[256,1024]{1,0:T(8,128)(2,1)} %param.9) | copy-start | bytes 1572868
  30.3 558.1 %reduce-scatter.2.cloned.1.call-start = ((), (), s32[]{:S(2)}) async-start(), calls=%async_computation.4 | async-start | bytes 5242880 | tf_op jit(solution)/shard_map/reduce_scatter | solution.py:33
  554.3 105.5 %copy-start.3 = (bf16[256,2048]{1,0:T(8,128)(2,1)S(1)}, bf16[256,2048]{1,0:T(8,128)(2,1)}, u32[]{:S(2)}) copy-start(bf16[256,2048]{1,0:T(8,128)(2,1)} %param.13) | copy-start | bytes 3145732
  606.3 57.1 %copy-start.5 = (f32[2048]{0:T(1024)}, f32[2048]{0:T(1024)S(1)}, u32[]{:S(2)}) copy-start(f32[2048]{0:T(1024)S(1)} %psum.22) | copy-start | bytes 24580
Sparse Core Ops, SparseCore 0:
  10.1 201.9 all-gather.5
  214.2 226.7 all-gather.3
  443.7 97.5 all-gather.7
  543.7 44.6 reduce-scatter.1
where the time goes:
time: 672 us; the launch traced here: 671 us
  waiting for transfers between devices  514 us (76%)
  blocking collectives  66.8 us (10%)
  matrix products  32.3 us (5%)
  other arithmetic  27 us (4%)
  between operations  17.6 us (3%)
    all_gather x1, waiting for transfers between devices, local(): lax.all_gather(w_query, 'row', axis=0, tiled=True)  220 us
    all_gather x1, waiting for transfers between devices, local(): lax.all_gather(w_keyval, 'row', axis=0, tiled=True)  182 us
    all_gather x1, waiting for transfers between devices, local(): all_cotangents = lax.all_gather(cotangent, 'row', axis=0, tiled=True)  81.3 us
    psum x1, blocking collectives, local(): grand_total = lax.psum(tile_square + leading, ('row', 'col'))  45.6 us
    reduce_scatter x1, waiting for transfers between devices, local(): lax.psum_scatter(rounded.astype(jnp.bfloat16), 'col', scatter_dimension=1...  29.9 us
    psum x1, blocking collectives, local(): grad_gain = lax.psum(gain_partial, 'row')  15.3 us
  transfers between devices with their start and end apart: 5, of which 4 were waited for; matrix products, arithmetic and copies ran while one was open for 9% of the time, Pallas kernels for 0%

commit v1 on v0

--- a/solution.py
+++ b/solution.py
@@ -71,7 +71,7 @@
     leading = jnp.where(
         lax.axis_index("row") == 0, jnp.sum(grad_gain * grad_gain), jnp.float32(0.0)
     )
-    grand_total = lax.psum(tile_square + leading, ("row", "col"))
+    grand_total = lax.psum(lax.psum(tile_square + leading, "row"), "col")
     grad_square_sum = grand_total / jnp.float32(model_width)
     return (d_input, grad_wq, grad_wkv, grad_gain, grad_square_sum)
 

time: 672 us -> 652 us (0.970)
  blocking collectives: 66.8 us -> 43.7 us
    psum x1, blocking collectives: 45.6 us -> 21.9 us  [local(): grand_total = lax.psum(lax.psum(tile_square + leading, 'row'), 'col')]
where the time goes in v1:
time: 652 us; the launch traced here: 648 us
  waiting for transfers between devices  514 us (79%)
  blocking collectives  43.7 us (7%)
  matrix products  32.3 us (5%)
  other arithmetic  27 us (4%)
  between operations  17.6 us (3%)
  local copies, waits for them, and re-layouts  6.69 us (1%)
    all_gather x1, waiting for transfers between devices, local(): lax.all_gather(w_query, 'row', axis=0, tiled=True)  220 us
    all_gather x1, waiting for transfers between devices, local(): lax.all_gather(w_keyval, 'row', axis=0, tiled=True)  182 us
    all_gather x1, waiting for transfers between devices, local(): all_cotangents = lax.all_gather(cotangent, 'row', axis=0, tiled=True)  81.3 us
    reduce_scatter x1, waiting for transfers between devices, local(): lax.psum_scatter(rounded.astype(jnp.bfloat16), 'col', scatter_dimension=1...  29.9 us
    psum x1, blocking collectives, local(): grand_total = lax.psum(lax.psum(tile_square + leading, 'row'), 'col')  21.9 us
    psum x1, blocking collectives, local(): grad_gain = lax.psum(gain_partial, 'row')  15.3 us
  transfers between devices with their start and end apart: 5, of which 4 were waited for; matrix products, arithmetic and copies ran while one was open for 9% of the time, Pallas kernels for 0%

profile of v1, /device:TPU:12, one launch (start us, length us, event | category | flops | bytes accessed | tf_op | source)
XLA Modules:
  0.0 647.9 jit_solution(7471728717102436733)
XLA Ops:
  7.2 0.0 all-gather.6.cloned.1.call-start
  7.2 0.7 all-gather.6.cloned.1.call-update
  7.9 0.0 copy-start.4
  7.9 0.0 all-gather.4.cloned.1.call-start
  8.0 0.7 all-gather.4.cloned.1.call-update
  8.7 0.0 all-gather.8.cloned.1.call-start
  8.7 2.1 pad_maximum_fusion
  10.8 0.0 all-gather.8.cloned.1.call-update
  10.8 0.0 copy-start
  10.8 3.3 multiply_reduce_fusion
  14.1 0.0 copy-done.4
  14.1 0.2 copy-done
  14.2 3.2 multiply_convert_fusion.1
  17.4 6.5 %copy.13 = bf16[256,8192]{0,1:T(8,128)(2,1)} copy(bf16[256,8192]{1,0:T(8,128)(2,1)} %multiply_convert_fusion.1) | data formatting | bytes 8388608 | tf_op jit(solution)/shard_map/all_to_all | solution.py:50
  23.9 0.0 copy-start.2
  23.9 6.4 all-to-all-start
  30.3 0.0 copy-start.1
  30.3 0.0 reduce-scatter.2.cloned.1.call-start
  30.3 181.7 %all-gather.6.cloned.1.call-done = bf16[8192,512]{1,0:T(8,128)(2,1)} async-done(((bf16[1024,512]{1,0:T(8,128)(2,1)}), bf16[8192,512]{1,0:T(8,128)(2,1)}) %all-gather.6.cloned.1.call-update) | async-done | bytes 8388624 | tf_op jit(solution)/shard_map/all_gather | solution.py:28
  212.0 0.0 copy-done.2
  212.0 9.0 %fusion.11 = f32[256,8192]{1,0:T(8,128)} fusion(bf16[256,512]{1,0:T(8,128)(2,1)S(1)} %copy-done.2, bf16[8192,512]{1,0:T(8,128)(2,1)} %all-gather.6.cloned.1.call-done), kind=kOutput, calls=%fused_computation.24 | convolution fusion | flops 2147483648 | bytes 17039360 | tf_op jit(solution)/shard_map/dot_general | solution.py:26
  221.0 219.9 %all-gather.4.cloned.1.call-done = bf16[8192,1024]{1,0:T(8,128)(2,1)} async-done(((bf16[1024,1024]{1,0:T(8,128)(2,1)}), bf16[8192,1024]{1,0:T(8,128)(2,1)}) %all-gather.4.cloned.1.call-update) | async-done | bytes 16777232 | tf_op jit(solution)/shard_map/all_gather | solution.py:22
  440.9 0.0 copy-done.1
  440.9 12.4 %fusion = bf16[256,8192]{1,0:T(8,128)(2,1)} fusion(f32[256,8192]{1,0:T(8,128)} %fusion.11, bf16[256,1024]{1,0:T(8,128)(2,1)S(1)} %copy-done.1, bf16[8192,1024]{1,0:T(8,128)(2,1)} %all-gather.4.cloned.1.call-done), kind=kOutput, calls=%fused_computation.2 | convolution fusion | flops 4299161600 | bytes 29884416 | tf_op jit(solution)/shard_map/dot_general | solution.py:20
  453.4 0.0 reduce-scatter.2.cloned.1.call-update
  453.4 6.7 %convert_element_type.35 = f32[256,8192]{1,0:T(8,128)} convert(bf16[256,8192]{1,0:T(8,128)(2,1)} %param.7) | non-fusion elementwise | flops 2097152 | bytes 12582912 | tf_op jit(solution)/shard_map/convert_element_type | solution.py:11
  460.0 0.0 all-to-all-done
  460.1 81.3 %all-gather.8.cloned.1.call-done = bf16[2048,1536]{1,0:T(8,128)(2,1)} async-done(((bf16[256,1536]{1,0:T(8,128)(2,1)}), bf16[2048,1536]{1,0:T(8,128)(2,1)}) %all-gather.8.cloned.1.call-update) | async-done | bytes 6291472 | tf_op jit(solution)/shard_map/all_gather | solution.py:51
  541.3 10.9 %fusion.1 = bf16[1024,1536]{1,0:T(8,128)(2,1)S(1)} fusion(bf16[8,256,1536]{2,1,0:T(8,128)(2,1)} %bitcast.11, bf16[256,8,1024]{0,2,1:T(8,128)(2,1)} %all-to-all-done), kind=kOutput, calls=%fused_computation.5 | convolution fusion | flops 6478626816 | bytes 13631488 | tf_op jit(solution)/shard_map/dot_general | solution.py:56
  552.2 2.0 multiply_reduce_fusion.2
  554.3 0.0 copy-start.3
  554.3 2.9 multiply_reduce_fusion.1
  558.5 29.9 %reduce-scatter.2.cloned.1.call-done = bf16[256,2048]{1,0:T(8,128)(2,1)} async-done(((bf16[256,8192]{1,0:T(8,128)(2,1)}), bf16[256,2048]{1,0:T(8,128)(2,1)}) %reduce-scatter.2.cloned.1.call-update) | async-done | bytes 1048592 | tf_op jit(solution)/shard_map/reduce_scatter | solution.py:33
  588.4 2.6 fusion.10
  591.0 15.3 %psum.29 = f32[2048]{0:T(1024)S(1)} all-reduce(f32[2048]{0:T(1024)S(1)} %broadcast_multiply_fusion), channel_id=1, replica_groups=mesh['row'=8,'col'=4] {'row'}, use_global_device_ids=true, to_apply=%region_6.0 | all-reduce | flops 2048 | bytes 16384 | tf_op jit(solution)/shard_map/psum | solution.py:70
  606.3 0.0 copy-start.5
  606.3 0.6 multiply_reduce_fusion.3
  607.5 21.9 %psum.30 = f32[]{:T(128)} all-reduce(f32[]{:T(128)S(6)} %add.46), channel_id=1, replica_groups=mesh['row'=8,'col'=4] {'row'}, use_global_device_ids=true, to_apply=%region_10.11 | all-reduce | flops 1 | bytes 8 | tf_op jit(solution)/shard_map/psum | solution.py:74
  629.4 6.5 %all-reduce = (f32[256]{0:T(256)S(1)}, f32[]{:T(128)}) all-reduce(f32[256]{0:T(256)S(1)} %get-tuple-element.6, f32[]{:T(128)} %psum.30), channel_id=1, replica_groups=mesh['row'=8,'col'=4] {'col'}, use_global_device_ids=true, to_apply=%region_3.0 | all-reduce | flops 257 | bytes 2056 | tf_op jit(solution)/shard_map/psum | solution.py:41
  636.6 0.0 copy-done.3
  636.6 3.6 fusion.7
  640.3 0.0 copy-done.5
  (3 shorter events, 0.0 us)
Async XLA Ops:
  7.2 204.9 %all-gather.6.cloned.1.call-start = ((), (), s32[]{:S(2)}) async-start(), calls=%async_computation.3 | async-start | bytes 9437184 | tf_op jit(solution)/shard_map/all_gather | solution.py:28
  7.9 6.2 copy-start.4
  7.9 433.0 %all-gather.4.cloned.1.call-start = ((), (), s32[]{:S(2)}) async-start(), calls=%async_computation.2 | async-start | bytes 18874368 | tf_op jit(solution)/shard_map/all_gather | solution.py:22
  8.7 532.6 %all-gather.8.cloned.1.call-start = ((), (), s32[]{:S(2)}) async-start(), calls=%async_computation.5 | async-start | bytes 7077888 | tf_op jit(solution)/shard_map/all_gather | solution.py:51
  10.8 3.5 copy-start
  23.9 188.1 %copy-start.2 = (bf16[256,512]{1,0:T(8,128)(2,1)S(1)}, bf16[256,512]{1,0:T(8,128)(2,1)}, u32[]{:S(2)}) copy-start(bf16[256,512]{1,0:T(8,128)(2,1)} %param.10) | copy-start | bytes 786436
  23.9 436.1 %all-to-all-start = ((bf16[256,8,1024]{0,2,1:T(8,128)(2,1)}), bf16[256,8,1024]{0,2,1:T(8,128)(2,1)}, u32[]{:S(2)}, u32[]{:S(2)}) async-start(bf16[256,8,1024]{0,2,1:T(8,128)(2,1)} %bitcast.10), calls=%async_computation.1 | async-start | bytes 8388608 | tf_op jit(solution)/shard_map/all_to_all | solution.py:50
  30.3 410.6 %copy-start.1 = (bf16[256,1024]{1,0:T(8,128)(2,1)S(1)}, bf16[256,1024]{1,0:T(8,128)(2,1)}, u32[]{:S(2)}) copy-start(bf16[256,1024]{1,0:T(8,128)(2,1)} %param.9) | copy-start | bytes 1572868
  30.3 558.1 %reduce-scatter.2.cloned.1.call-start = ((), (), s32[]{:S(2)}) async-start(), calls=%async_computation.4 | async-start | bytes 5242880 | tf_op jit(solution)/shard_map/reduce_scatter | solution.py:33
  554.3 82.3 %copy-start.3 = (bf16[256,2048]{1,0:T(8,128)(2,1)S(1)}, bf16[256,2048]{1,0:T(8,128)(2,1)}, u32[]{:S(2)}) copy-start(bf16[256,2048]{1,0:T(8,128)(2,1)} %param.13) | copy-start | bytes 3145732
  606.3 34.0 %copy-start.5 = (f32[2048]{0:T(1024)}, f32[2048]{0:T(1024)S(1)}, u32[]{:S(2)}) copy-start(f32[2048]{0:T(1024)S(1)} %psum.29) | copy-start | bytes 24580
Sparse Core Ops, SparseCore 0:
  10.1 201.9 all-gather.5
  214.2 226.7 all-gather.3
  443.7 97.5 all-gather.7
  543.7 44.6 reduce-scatter.1
